TPU v7x, 32 devices: a whole 2x2x4 slice. The times are simulated.
32 devices in a mesh: gx: 2 (over y), gy: 4 (over z), gz: 4 (over x, core).
Axes of the slice: x: 2, y: 2, z: 4, core: 2. Of those that a mesh axis runs over, the one named last changes fastest.
Arguments:
- blocks: bfloat16 [1600, 64, 4096], P(('gx', 'gy', 'gz')), may hold values from -6 to 6
- ownership: int32 [1600, 3], P(('gx', 'gy', 'gz')), may hold values from -1 to 15, as said below
- basis_rows: bfloat16 [1024, 48], replicated, may hold values from -0.1875 to 0.1875
Outputs:
- gram_matrix: float32 [1024, 1024], P(('gx', 'gy', 'gz'))
Inputs may be any that keep to these rules, and one draw needn't show every extreme that they name: `ownership`: row d * 50 + s is slot s of device d in mesh order. Each row is a block triple (i, j, k) with i <= j <= k, or -1 -1 -1 for an empty slot; every such triple of blocks 0 to 15 stands in exactly one row; the live slots of a device come first; some device has all 50 slots live.
All inputs are finite; a program needn't handle non-finite values.
Results may differ from a plain program's by a relative error of at most 0.0037.
Values may be sent and summed in bfloat16 or wider, within the bound.
A program may use at most 192 MiB of HBM per device.

v0:
```python
import jax
import jax.numpy as jnp
from jax import lax
from jax.sharding import PartitionSpec as P

AXES = ("gx", "gy", "gz")
GROUP = 10


def element_weights(triples, extent):
    shape = (1, extent, extent, extent)
    x = lax.broadcasted_iota(jnp.int32, shape, 1)
    y = lax.broadcasted_iota(jnp.int32, shape, 2)
    z = lax.broadcasted_iota(jnp.int32, shape, 3)

    def per_slot(flag):
        return flag[:, None, None, None]

    front = per_slot(triples[:, 0] < triples[:, 1])
    back = per_slot(triples[:, 1] < triples[:, 2])
    live = per_slot(triples[:, 0] >= 0)
    sorted_place = live & (front | (x <= y)) & (back | (y <= z))
    front_strict = front | (x < y)
    back_strict = back | (y < z)
    zero = jnp.bfloat16(0)
    half = jnp.bfloat16(0.5)
    one = jnp.bfloat16(1)
    first = jnp.where(sorted_place, jnp.where(back_strict, one, half), zero)
    second = jnp.where(sorted_place & front_strict, one, zero)
    third = jnp.where(
        sorted_place & back_strict, jnp.where(front_strict, one, half), zero
    )
    return first, second, third


def local(blocks, ownership, basis_rows):
    slots, extent, _ = blocks.shape
    size, rank = basis_rows.shape
    block_rows = size // extent
    basis_blocks = basis_rows.reshape(block_rows, extent, rank)
    group = min(GROUP, slots)
    turns = (slots + group - 1) // group

    def add_group(turn, total):
        first_slot = jnp.minimum(turn * group, slots - group)
        stored = lax.dynamic_slice_in_dim(blocks, first_slot, group, 0)
        triples = lax.dynamic_slice_in_dim(ownership, first_slot, group, 0)
        fresh = first_slot + jnp.arange(group, dtype=jnp.int32) >= turn * group
        triples = jnp.where(fresh[:, None], triples, -1)
        tensor = stored.reshape(group, extent, extent, extent)
        w0, w1, w2 = element_weights(triples, extent)
        own = (triples[:, :, None] == jnp.arange(block_rows, dtype=jnp.int32)).astype(jnp.bfloat16)
        factors = jnp.take(basis_blocks, jnp.clip(triples, 0, block_rows - 1), axis=0)
        f0, f1, f2 = factors[:, 0], factors[:, 1], factors[:, 2]

        def reduce(form, weights, factor):
            return jnp.einsum(
                form, tensor * weights, factor, preferred_element_type=jnp.float32
            ).astype(jnp.bfloat16)

        def left(position, factor):
            return own[:, position, None, :, None] * factor[:, :, None, :]

        rows0 = reduce("gxyz,gzq->gyqx", w0, f2)
        rows1 = reduce("gxyz,gzq->gxqy", w1, f2)
        rows2 = reduce("gxyz,gyq->gxqz", w2, f1)
        sides = jnp.concatenate([left(0, f1), left(1, f0), left(2, f0)], axis=0)
        rows = jnp.concatenate([rows0, rows1, rows2], axis=0)
        return total + jnp.einsum(
            "gbnp,gbqa->npqa", sides, rows, preferred_element_type=jnp.float32
        )

    zero_rows = jnp.zeros((block_rows, rank, rank, extent), jnp.float32)
    total = lax.fori_loop(0, turns, add_group, zero_rows)
    paired = total + jnp.swapaxes(total, 1, 2)
    low = rank // 2
    top = paired[:, :low].reshape(block_rows, low * rank, extent)
    corner = paired[:, low:, low:].reshape(block_rows, (rank - low) ** 2, extent)
    packed = jnp.concatenate([top, corner], axis=1).astype(jnp.bfloat16)
    packed = jnp.swapaxes(packed, 1, 2).reshape(size, -1)
    devices = lax.axis_size(AXES)
    pieces = lax.all_to_all(
        packed.reshape(devices, size // devices, -1), AXES, split_axis=0, concat_axis=0, tiled=True
    )
    rounded = jnp.sum(pieces.astype(jnp.float32), axis=0).astype(jnp.bfloat16)
    column = lax.broadcasted_iota(jnp.int32, (1, rounded.shape[1]), 1)
    crossed = (column < low * rank) & (lax.rem(column, rank) >= low)
    doubled = jnp.where(crossed, rounded * jnp.bfloat16(2), rounded)
    gram_rows = lax.dot_general(
        doubled,
        lax.all_gather(rounded, AXES, axis=0, tiled=True),
        (((1,), (1,)), ((), ())),
        preferred_element_type=jnp.float32,
    )
    return gram_rows / rank


def solution(mesh):
    in_specs = (P(AXES, None, None), P(AXES, None), P())
    out_specs = P(AXES, None)
    return jax.shard_map(local, mesh=mesh, in_specs=in_specs, out_specs=out_specs, check_vma=False)
```

profile of v0, /device:TPU:0, one launch (start us, length us, event | category | flops | bytes accessed | tf_op | source)
XLA Modules:
  0.0 815.1 jit_solution(9107928555283585652)
XLA Ops:
  8.3 599.6 %while.14 = (s32[]{:T(128)}, f32[16,48,48,64]{3,1,2,0:T(8,128)}, s32[50,3]{0,1:T(4,128)}, bf16[16,64,48]{2,1,0:T(8,128)(2,1)}, bf16[50,64,4096]{2,1,0:T(8,128)(2...) while((s32[]{:T(128)}, f32[16,48,48,64]{3,1,2,0:T(8,128)}, ...), condition=%wide.region_1.2_spmd.clone, body=%wide.region_0.1_spmd.clone.sunk | while | flops 9957994496 | bytes 116283336 | solution.py:74
  16.6 15.2 %reshape.145 = bf16[10,64,64,64]{3,2,1,0:T(8,128)(2,1)} reshape(bf16[10,64,4096]{2,1,0:T(8,128)(2,1)} %constant_dynamic-slice_fusion.2) | data formatting | bytes 10485760 | tf_op jit(solution)/shard_map/while/body/eval_jaxpr/reshape | solution.py:50
  33.2 12.7 %fusion.71 = bf16[10,48,64,64]{3,1,2,0:T(8,128)(2,1)S(1)} fusion(bf16[10,64,64,64]{3,2,1,0:T(8,128)(2,1)} %reshape.145, pred[64,64,64]{2,1,0:T(8,128)(4,1)S(1)} %get-tuple-element.193, pred[10]{0:T(512)(128)(4,1)S(1)} %get-tuple-element.197, bf16[10,3,64,48]{2,3,0,1:T(8,128)(2,1)S(1)} %broadcast_select_fusion.2, ...), kind=kOutput, calls=%fused_computation.18.clone.1 | convolution fusion | flops 280494080 | bytes 10872320 | tf_op jit(solution)/shard_map/while/body/eval_jaxpr/gxyz,gzq->gxqy/dot_general | solution.py:57
  51.1 14.8 %fusion.72 = bf16[10,48,64,64]{3,1,2,0:T(8,128)(2,1)} fusion(bf16[10,64,64,64]{3,2,1,0:T(8,128)(2,1)} %reshape.145, pred[64,64,64]{2,1,0:T(8,128)(4,1)} %get-tuple-element.194, pred[10]{0:T(512)(128)(4,1)S(1)} %get-tuple-element.196, bf16[10,3,64,48]{2,3,0,1:T(8,128)(2,1)S(1)} %broadcast_select_fusion.2, pred[10]{0:T(512)(128)(4,1)S(1)} %get-tuple-element.199, ...), kind=kOutput, calls=%fused_computation.23.clone.1 | convolution fusion | flops 280494080 | bytes 10610176 | tf_op jit(solution)/shard_map/while/body/eval_jaxpr/gxyz,gzq->gyqx/dot_general | solution.py:57
  66.0 11.2 %copy.40 = bf16[10,48,64,64]{2,3,0,1:T(8,128)(2,1)} copy(bf16[10,48,64,64]{3,1,2,0:T(8,128)(2,1)} %fusion.72) | data formatting | bytes 7864320 | tf_op jit(solution)/shard_map/while/body/eval_jaxpr/gxyz,gzq->gyqx/dot_general | solution.py:57
  77.2 14.7 %fusion.70 = bf16[10,48,64,64]{3,1,2,0:T(8,128)(2,1)S(1)} fusion(bf16[10,64,64,64]{3,2,1,0:T(8,128)(2,1)} %reshape.145, pred[64,64,64]{2,1,0:T(8,128)(4,1)S(1)} %get-tuple-element.193, pred[64,64,64]{2,1,0:T(8,128)(4,1)} %get-tuple-element.194, pred[10]{0:T(512)(128)(4,1)S(1)} %get-tuple-element.196, pred[10]{0:T(512)(128)(4,1)S(1)} %get-tuple-element.197, ...), kind=kOutput, calls=%fused_computation.20.clone.1 | convolution fusion | flops 285736960 | bytes 11134464 | tf_op jit(solution)/shard_map/while/body/eval_jaxpr/gxyz,gyq->gxqz/dot_general | solution.py:57
  99.5 27.3 %bitcast_add_fusion.3 = f32[16,48,48,64]{3,1,2,0:T(8,128)} fusion(f32[16,48,48,64]{3,1,2,0:T(8,128)} %get-tuple-element.221, pred[]{:T(512)S(6)} %compare.3, bf16[10,64,48,64]{3,1,0,2:T(8,128)(2,1)} %bitcast.93, bf16[10,64,48,64]{3,1,0,2:T(8,128)(2,1)} %bitcast.91, bf16[10,64,48,64]{3,1,0,2:T(8,128)(2,1)} %bitcast.92, ...), kind=kOutput, calls=%fused_computation.14.clone.1 | convolution fusion | flops 9108652032 | bytes 33619968 | tf_op jit(solution)/shard_map/while/body/eval_jaxpr/gbnp,gbqa->npqa/dot_general | solution.py:69
  135.1 15.2 %reshape.145 = bf16[10,64,64,64]{3,2,1,0:T(8,128)(2,1)} reshape(bf16[10,64,4096]{2,1,0:T(8,128)(2,1)} %constant_dynamic-slice_fusion.2) | data formatting | bytes 10485760 | tf_op jit(solution)/shard_map/while/body/eval_jaxpr/reshape | solution.py:50
  151.6 12.7 %fusion.71 = bf16[10,48,64,64]{3,1,2,0:T(8,128)(2,1)S(1)} fusion(bf16[10,64,64,64]{3,2,1,0:T(8,128)(2,1)} %reshape.145, pred[64,64,64]{2,1,0:T(8,128)(4,1)S(1)} %get-tuple-element.193, pred[10]{0:T(512)(128)(4,1)S(1)} %get-tuple-element.197, bf16[10,3,64,48]{2,3,0,1:T(8,128)(2,1)S(1)} %broadcast_select_fusion.2, ...), kind=kOutput, calls=%fused_computation.18.clone.1 | convolution fusion | flops 280494080 | bytes 10872320 | tf_op jit(solution)/shard_map/while/body/eval_jaxpr/gxyz,gzq->gxqy/dot_general | solution.py:57
  169.6 14.8 %fusion.72 = bf16[10,48,64,64]{3,1,2,0:T(8,128)(2,1)} fusion(bf16[10,64,64,64]{3,2,1,0:T(8,128)(2,1)} %reshape.145, pred[64,64,64]{2,1,0:T(8,128)(4,1)} %get-tuple-element.194, pred[10]{0:T(512)(128)(4,1)S(1)} %get-tuple-element.196, bf16[10,3,64,48]{2,3,0,1:T(8,128)(2,1)S(1)} %broadcast_select_fusion.2, pred[10]{0:T(512)(128)(4,1)S(1)} %get-tuple-element.199, ...), kind=kOutput, calls=%fused_computation.23.clone.1 | convolution fusion | flops 280494080 | bytes 10610176 | tf_op jit(solution)/shard_map/while/body/eval_jaxpr/gxyz,gzq->gyqx/dot_general | solution.py:57
  184.4 11.2 %copy.40 = bf16[10,48,64,64]{2,3,0,1:T(8,128)(2,1)} copy(bf16[10,48,64,64]{3,1,2,0:T(8,128)(2,1)} %fusion.72) | data formatting | bytes 7864320 | tf_op jit(solution)/shard_map/while/body/eval_jaxpr/gxyz,gzq->gyqx/dot_general | solution.py:57
  195.6 14.7 %fusion.70 = bf16[10,48,64,64]{3,1,2,0:T(8,128)(2,1)S(1)} fusion(bf16[10,64,64,64]{3,2,1,0:T(8,128)(2,1)} %reshape.145, pred[64,64,64]{2,1,0:T(8,128)(4,1)S(1)} %get-tuple-element.193, pred[64,64,64]{2,1,0:T(8,128)(4,1)} %get-tuple-element.194, pred[10]{0:T(512)(128)(4,1)S(1)} %get-tuple-element.196, pred[10]{0:T(512)(128)(4,1)S(1)} %get-tuple-element.197, ...), kind=kOutput, calls=%fused_computation.20.clone.1 | convolution fusion | flops 285736960 | bytes 11134464 | tf_op jit(solution)/shard_map/while/body/eval_jaxpr/gxyz,gyq->gxqz/dot_general | solution.py:57
  217.9 29.1 %bitcast_add_fusion.3 = f32[16,48,48,64]{3,1,2,0:T(8,128)} fusion(f32[16,48,48,64]{3,1,2,0:T(8,128)} %get-tuple-element.221, pred[]{:T(512)S(6)} %compare.3, bf16[10,64,48,64]{3,1,0,2:T(8,128)(2,1)} %bitcast.93, bf16[10,64,48,64]{3,1,0,2:T(8,128)(2,1)} %bitcast.91, bf16[10,64,48,64]{3,1,0,2:T(8,128)(2,1)} %bitcast.92, ...), kind=kOutput, calls=%fused_computation.14.clone.1 | convolution fusion | flops 9108652032 | bytes 33619968 | tf_op jit(solution)/shard_map/while/body/eval_jaxpr/gbnp,gbqa->npqa/dot_general | solution.py:69
  255.4 15.2 %reshape.145 = bf16[10,64,64,64]{3,2,1,0:T(8,128)(2,1)} reshape(bf16[10,64,4096]{2,1,0:T(8,128)(2,1)} %constant_dynamic-slice_fusion.2) | data formatting | bytes 10485760 | tf_op jit(solution)/shard_map/while/body/eval_jaxpr/reshape | solution.py:50
  271.9 12.7 %fusion.71 = bf16[10,48,64,64]{3,1,2,0:T(8,128)(2,1)S(1)} fusion(bf16[10,64,64,64]{3,2,1,0:T(8,128)(2,1)} %reshape.145, pred[64,64,64]{2,1,0:T(8,128)(4,1)S(1)} %get-tuple-element.193, pred[10]{0:T(512)(128)(4,1)S(1)} %get-tuple-element.197, bf16[10,3,64,48]{2,3,0,1:T(8,128)(2,1)S(1)} %broadcast_select_fusion.2, ...), kind=kOutput, calls=%fused_computation.18.clone.1 | convolution fusion | flops 280494080 | bytes 10872320 | tf_op jit(solution)/shard_map/while/body/eval_jaxpr/gxyz,gzq->gxqy/dot_general | solution.py:57
  289.9 14.8 %fusion.72 = bf16[10,48,64,64]{3,1,2,0:T(8,128)(2,1)} fusion(bf16[10,64,64,64]{3,2,1,0:T(8,128)(2,1)} %reshape.145, pred[64,64,64]{2,1,0:T(8,128)(4,1)} %get-tuple-element.194, pred[10]{0:T(512)(128)(4,1)S(1)} %get-tuple-element.196, bf16[10,3,64,48]{2,3,0,1:T(8,128)(2,1)S(1)} %broadcast_select_fusion.2, pred[10]{0:T(512)(128)(4,1)S(1)} %get-tuple-element.199, ...), kind=kOutput, calls=%fused_computation.23.clone.1 | convolution fusion | flops 280494080 | bytes 10610176 | tf_op jit(solution)/shard_map/while/body/eval_jaxpr/gxyz,gzq->gyqx/dot_general | solution.py:57
  304.7 11.2 %copy.40 = bf16[10,48,64,64]{2,3,0,1:T(8,128)(2,1)} copy(bf16[10,48,64,64]{3,1,2,0:T(8,128)(2,1)} %fusion.72) | data formatting | bytes 7864320 | tf_op jit(solution)/shard_map/while/body/eval_jaxpr/gxyz,gzq->gyqx/dot_general | solution.py:57
  315.9 14.7 %fusion.70 = bf16[10,48,64,64]{3,1,2,0:T(8,128)(2,1)S(1)} fusion(bf16[10,64,64,64]{3,2,1,0:T(8,128)(2,1)} %reshape.145, pred[64,64,64]{2,1,0:T(8,128)(4,1)S(1)} %get-tuple-element.193, pred[64,64,64]{2,1,0:T(8,128)(4,1)} %get-tuple-element.194, pred[10]{0:T(512)(128)(4,1)S(1)} %get-tuple-element.196, pred[10]{0:T(512)(128)(4,1)S(1)} %get-tuple-element.197, ...), kind=kOutput, calls=%fused_computation.20.clone.1 | convolution fusion | flops 285736960 | bytes 11134464 | tf_op jit(solution)/shard_map/while/body/eval_jaxpr/gxyz,gyq->gxqz/dot_general | solution.py:57
  338.2 29.1 %bitcast_add_fusion.3 = f32[16,48,48,64]{3,1,2,0:T(8,128)} fusion(f32[16,48,48,64]{3,1,2,0:T(8,128)} %get-tuple-element.221, pred[]{:T(512)S(6)} %compare.3, bf16[10,64,48,64]{3,1,0,2:T(8,128)(2,1)} %bitcast.93, bf16[10,64,48,64]{3,1,0,2:T(8,128)(2,1)} %bitcast.91, bf16[10,64,48,64]{3,1,0,2:T(8,128)(2,1)} %bitcast.92, ...), kind=kOutput, calls=%fused_computation.14.clone.1 | convolution fusion | flops 9108652032 | bytes 33619968 | tf_op jit(solution)/shard_map/while/body/eval_jaxpr/gbnp,gbqa->npqa/dot_general | solution.py:69
  375.7 15.2 %reshape.145 = bf16[10,64,64,64]{3,2,1,0:T(8,128)(2,1)} reshape(bf16[10,64,4096]{2,1,0:T(8,128)(2,1)} %constant_dynamic-slice_fusion.2) | data formatting | bytes 10485760 | tf_op jit(solution)/shard_map/while/body/eval_jaxpr/reshape | solution.py:50
  392.2 12.7 %fusion.71 = bf16[10,48,64,64]{3,1,2,0:T(8,128)(2,1)S(1)} fusion(bf16[10,64,64,64]{3,2,1,0:T(8,128)(2,1)} %reshape.145, pred[64,64,64]{2,1,0:T(8,128)(4,1)S(1)} %get-tuple-element.193, pred[10]{0:T(512)(128)(4,1)S(1)} %get-tuple-element.197, bf16[10,3,64,48]{2,3,0,1:T(8,128)(2,1)S(1)} %broadcast_select_fusion.2, ...), kind=kOutput, calls=%fused_computation.18.clone.1 | convolution fusion | flops 280494080 | bytes 10872320 | tf_op jit(solution)/shard_map/while/body/eval_jaxpr/gxyz,gzq->gxqy/dot_general | solution.py:57
  410.2 14.8 %fusion.72 = bf16[10,48,64,64]{3,1,2,0:T(8,128)(2,1)} fusion(bf16[10,64,64,64]{3,2,1,0:T(8,128)(2,1)} %reshape.145, pred[64,64,64]{2,1,0:T(8,128)(4,1)} %get-tuple-element.194, pred[10]{0:T(512)(128)(4,1)S(1)} %get-tuple-element.196, bf16[10,3,64,48]{2,3,0,1:T(8,128)(2,1)S(1)} %broadcast_select_fusion.2, pred[10]{0:T(512)(128)(4,1)S(1)} %get-tuple-element.199, ...), kind=kOutput, calls=%fused_computation.23.clone.1 | convolution fusion | flops 280494080 | bytes 10610176 | tf_op jit(solution)/shard_map/while/body/eval_jaxpr/gxyz,gzq->gyqx/dot_general | solution.py:57
  436.2 14.7 %fusion.70 = bf16[10,48,64,64]{3,1,2,0:T(8,128)(2,1)S(1)} fusion(bf16[10,64,64,64]{3,2,1,0:T(8,128)(2,1)} %reshape.145, pred[64,64,64]{2,1,0:T(8,128)(4,1)S(1)} %get-tuple-element.193, pred[64,64,64]{2,1,0:T(8,128)(4,1)} %get-tuple-element.194, pred[10]{0:T(512)(128)(4,1)S(1)} %get-tuple-element.196, pred[10]{0:T(512)(128)(4,1)S(1)} %get-tuple-element.197, ...), kind=kOutput, calls=%fused_computation.20.clone.1 | convolution fusion | flops 285736960 | bytes 11134464 | tf_op jit(solution)/shard_map/while/body/eval_jaxpr/gxyz,gyq->gxqz/dot_general | solution.py:57
  458.5 29.1 %bitcast_add_fusion.3 = f32[16,48,48,64]{3,1,2,0:T(8,128)} fusion(f32[16,48,48,64]{3,1,2,0:T(8,128)} %get-tuple-element.221, pred[]{:T(512)S(6)} %compare.3, bf16[10,64,48,64]{3,1,0,2:T(8,128)(2,1)} %bitcast.93, bf16[10,64,48,64]{3,1,0,2:T(8,128)(2,1)} %bitcast.91, bf16[10,64,48,64]{3,1,0,2:T(8,128)(2,1)} %bitcast.92, ...), kind=kOutput, calls=%fused_computation.14.clone.1 | convolution fusion | flops 9108652032 | bytes 33619968 | tf_op jit(solution)/shard_map/while/body/eval_jaxpr/gbnp,gbqa->npqa/dot_general | solution.py:69
  496.0 15.2 %reshape.145 = bf16[10,64,64,64]{3,2,1,0:T(8,128)(2,1)} reshape(bf16[10,64,4096]{2,1,0:T(8,128)(2,1)} %constant_dynamic-slice_fusion.2) | data formatting | bytes 10485760 | tf_op jit(solution)/shard_map/while/body/eval_jaxpr/reshape | solution.py:50
  512.5 12.7 %fusion.71 = bf16[10,48,64,64]{3,1,2,0:T(8,128)(2,1)S(1)} fusion(bf16[10,64,64,64]{3,2,1,0:T(8,128)(2,1)} %reshape.145, pred[64,64,64]{2,1,0:T(8,128)(4,1)S(1)} %get-tuple-element.193, pred[10]{0:T(512)(128)(4,1)S(1)} %get-tuple-element.197, bf16[10,3,64,48]{2,3,0,1:T(8,128)(2,1)S(1)} %broadcast_select_fusion.2, ...), kind=kOutput, calls=%fused_computation.18.clone.1 | convolution fusion | flops 280494080 | bytes 10872320 | tf_op jit(solution)/shard_map/while/body/eval_jaxpr/gxyz,gzq->gxqy/dot_general | solution.py:57
  530.5 14.8 %fusion.72 = bf16[10,48,64,64]{3,1,2,0:T(8,128)(2,1)} fusion(bf16[10,64,64,64]{3,2,1,0:T(8,128)(2,1)} %reshape.145, pred[64,64,64]{2,1,0:T(8,128)(4,1)} %get-tuple-element.194, pred[10]{0:T(512)(128)(4,1)S(1)} %get-tuple-element.196, bf16[10,3,64,48]{2,3,0,1:T(8,128)(2,1)S(1)} %broadcast_select_fusion.2, pred[10]{0:T(512)(128)(4,1)S(1)} %get-tuple-element.199, ...), kind=kOutput, calls=%fused_computation.23.clone.1 | convolution fusion | flops 280494080 | bytes 10610176 | tf_op jit(solution)/shard_map/while/body/eval_jaxpr/gxyz,gzq->gyqx/dot_general | solution.py:57
  556.5 14.7 %fusion.70 = bf16[10,48,64,64]{3,1,2,0:T(8,128)(2,1)S(1)} fusion(bf16[10,64,64,64]{3,2,1,0:T(8,128)(2,1)} %reshape.145, pred[64,64,64]{2,1,0:T(8,128)(4,1)S(1)} %get-tuple-element.193, pred[64,64,64]{2,1,0:T(8,128)(4,1)} %get-tuple-element.194, pred[10]{0:T(512)(128)(4,1)S(1)} %get-tuple-element.196, pred[10]{0:T(512)(128)(4,1)S(1)} %get-tuple-element.197, ...), kind=kOutput, calls=%fused_computation.20.clone.1 | convolution fusion | flops 285736960 | bytes 11134464 | tf_op jit(solution)/shard_map/while/body/eval_jaxpr/gxyz,gyq->gxqz/dot_general | solution.py:57
  578.8 29.1 %bitcast_add_fusion.3 = f32[16,48,48,64]{3,1,2,0:T(8,128)} fusion(f32[16,48,48,64]{3,1,2,0:T(8,128)} %get-tuple-element.221, pred[]{:T(512)S(6)} %compare.3, bf16[10,64,48,64]{3,1,0,2:T(8,128)(2,1)} %bitcast.93, bf16[10,64,48,64]{3,1,0,2:T(8,128)(2,1)} %bitcast.91, bf16[10,64,48,64]{3,1,0,2:T(8,128)(2,1)} %bitcast.92, ...), kind=kOutput, calls=%fused_computation.14.clone.1 | convolution fusion | flops 9108652032 | bytes 33619968 | tf_op jit(solution)/shard_map/while/body/eval_jaxpr/gbnp,gbqa->npqa/dot_general | solution.py:69
  607.9 15.7 %fusion.51 = bf16[16,48,48,64]{3,1,2,0:T(8,128)(2,1)S(1)} fusion(f32[16,48,48,64]{3,1,2,0:T(8,128)} %get-tuple-element.99), kind=kLoop, calls=%fused_computation.85 | loop fusion | flops 4718592 | bytes 14155776 | tf_op jit(solution)/shard_map/convert.6
  652.3 90.6 %all_to_all.5 = bf16[32,32,1728]{2,1,0:T(8,128)(2,1)} all-to-all(bf16[32,32,1728]{2,1,0:T(8,128)(2,1)S(1)} %bitcast.95), channel_id=1, replica_groups=mesh['gx'=2,'gy'=4,'gz'=4] {'gx','gy','gz'}, dimensions={0} | all-to-all | bytes 7077888 | tf_op jit(solution)/shard_map/all_to_all | solution.py:82
  746.2 58.2 %all-gather.2.cloned.1.call-done = bf16[1024,1728]{1,0:T(8,128)(2,1)} async-done(((bf16[32,1728]{1,0:T(8,128)(2,1)}), bf16[1024,1728]{1,0:T(8,128)(2,1)}) %all-gather.2.cloned.1.call-update) | async-done | bytes 3538960 | tf_op jit(solution)/shard_map/all_gather | solution.py:91
  (111 shorter events, 172.3 us)
Async XLA Ops:
  6.5 797.8 %all-gather.2.cloned.1.call-start = ((), (), s32[]{:S(2)}) async-start(), calls=%async_computation.1 | async-start | bytes 3784704 | tf_op jit(solution)/shard_map/all_gather | solution.py:91
Sparse Core Ops, SparseCore 0:
  746.3 58.0 all-gather.1
where the time goes:
time: 819 us; the launch traced here: 815 us
  matrix products  359 us (44%)
  local copies, waits for them, and re-layouts  250 us (31%)
  blocking collectives  90.6 us (11%)
  waiting for transfers between devices  58.2 us (7%)
  other arithmetic  43.4 us (5%)
  between operations  13.4 us (2%)
    dot_general x15, matrix products, reduce(): jnp.einsum(form, tensor * weights, factor, preferred_element_type=jnp.flo...  211 us
    dot_general x5, matrix products, add_group(): jnp.einsum('gbnp,gbqa->npqa', sides, rows, preferred_element_type=jnp.flo...  144 us
    dot_general x15, local copies, waits for them, and re-layouts, reduce(): jnp.einsum(form, tensor * weights, factor, preferred_element_type=jnp.flo...  109 us
    all_to_all x1, blocking collectives, local(): lax.all_to_all(packed.reshape(devices, size // devices, -1), AXES, split_...  90.6 us
    reshape x5, local copies, waits for them, and re-layouts, add_group(): tensor = stored.reshape(group, extent, extent, extent)  76.1 us
    all_gather x1, waiting for transfers between devices, local(): lax.all_gather(rounded, AXES, axis=0, tiled=True)  58.2 us
    dynamic_slice x5, local copies, waits for them, and re-layouts, add_group(): stored = lax.dynamic_slice_in_dim(blocks, first_slot, group, 0)  27.1 us
  transfers between devices with their start and end apart: 1, of which 1 were waited for; matrix products, arithmetic and copies ran while one was open for 0% of the time, Pallas kernels for 0%

commit v1 on v0

v1 whole, which is shorter than its diff:
```python
import functools

import jax
import jax.numpy as jnp
from jax import lax
from jax.experimental import pallas as pl
from jax.experimental.pallas import tpu as pltpu
from jax.sharding import PartitionSpec as P

AXES = ("gx", "gy", "gz")
DEPTH = 3
f32, bf16 = jnp.float32, jnp.bfloat16
MESH = pl.DeviceIdType.MESH


def contract_kernel(nb, ext, rank, own, count, blocks, ut, utp, ub, out, accv, accw, buf, sems, bd, mask, sv, sw, vb, pk, turning):
    half = ext // 2
    pitch = half + 1
    width = 4 * ext
    chunks = ext * ext // width
    low_rank = rank // 2
    n = count[0]

    def fetch(s):
        return pltpu.make_async_copy(blocks.at[s], buf.at[lax.rem(s, DEPTH)], sems.at[lax.rem(s, DEPTH)])

    for s in range(DEPTH - 1):
        @pl.when(s < n)
        def _():
            fetch(s).start()

    lane = lax.broadcasted_iota(jnp.int32, (ext, width), 1)
    row = lax.broadcasted_iota(jnp.int32, (ext, width), 0)

    def prepare(b, _):
        u = ub[b]
        u4 = jnp.concatenate([u, u, u, u], axis=1)
        for y in range(4):
            bd[b, y * ext:(y + 1) * ext, :] = jnp.where(lane // ext == y, u4, 0)
        accv[b] = jnp.zeros(accv.shape[1:], f32)
        accw[b] = jnp.zeros(accw.shape[1:], f32)
        return 0

    lax.fori_loop(0, nb, prepare, 0)

    for c in range(chunks):
        y = lane // ext + 4 * c
        z = lax.rem(lane, ext)
        front = jnp.where(row < y, 1.0, jnp.where(row == y, 0.5, 0.0))
        back = jnp.where(y < z, 1.0, jnp.where(y == z, 0.5, 0.0))
        both = jnp.where((row == y) & (y == z), 1.0 / 6.0, front * back)
        cols = slice(c * width, (c + 1) * width)
        mask[0, :, cols] = front.astype(bf16)
        mask[1, :, cols] = back.astype(bf16)
        mask[2, :, cols] = both.astype(bf16)

    def halves(a, b):
        low = lax.broadcasted_iota(jnp.int32, a.shape, 1) < ext
        return jnp.where(low, a, pltpu.roll(b, ext, 1)), jnp.where(low, pltpu.roll(a, ext, 1), b)

    def gather(src, first):
        e0, e1 = halves(src[pl.ds(first * pitch, half), :], src[pl.ds((first + 1) * pitch, half), :])
        return jnp.concatenate([e0, e1], axis=0).astype(bf16)

    def step(s, _):
        cur = lax.rem(s, DEPTH)
        fetch(s).wait()

        @pl.when(s + DEPTH - 1 < n)
        def _():
            fetch(s + DEPTH - 1).start()

        i, j, k = own[3 * s], own[3 * s + 1], own[3 * s + 2]
        kind = jnp.where(j == k, jnp.where(i == j, 2, 1), 0)

        @pl.when((i == j) | (j == k))
        def _():
            for c in range(chunks):
                cols = slice(c * width, (c + 1) * width)
                buf[cur, :, cols] = buf[cur, :, cols] * mask[kind, :, cols]

        ui = ut[i]
        uj = utp[j]
        bdk = bd[k]
        for c in range(chunks):
            cols = slice(c * width, (c + 1) * width)
            t = buf[cur, :, cols]
            v = jnp.dot(t, bdk, preferred_element_type=f32)
            sv[pl.ds(2 * c, ext, stride=pitch), :] = v[:, :128]
            sv[pl.ds(2 * c + 1, ext, stride=pitch), :] = v[:, 128:]
            vb[:, cols] = v.astype(bf16)
            w = jnp.dot(ui, t, preferred_element_type=f32)
            sw[pl.ds(2 * c, rank, stride=pitch), :] = w[:, :128]
            sw[pl.ds(2 * c + 1, rank, stride=pitch), :] = w[:, 128:]
        for c in range(chunks):
            cols = slice(c * width, (c + 1) * width)
            accv[j, :, cols] += jnp.dot(ui, vb[:, cols], preferred_element_type=f32)
        for c in range(chunks):
            cols = slice(c * width, (c + 1) * width)
            e = jnp.concatenate([gather(sv, 4 * c), gather(sv, 4 * c + 2)], axis=1)
            accv[i, :, cols] += jnp.dot(uj, e, preferred_element_type=f32)
        for c in range(rank * ext // width):
            cols = slice(c * width, (c + 1) * width)
            e = jnp.concatenate([gather(sw, 4 * c), gather(sw, 4 * c + 2)], axis=1)
            accw[k, :, cols] += jnp.dot(uj, e, preferred_element_type=f32)
        return 0

    lax.fori_loop(0, n, step, 0)

    def spread(x, b):
        l = lax.rem(lax.broadcasted_iota(jnp.int32, x.shape, 1), ext)
        if b < 2:
            return pltpu.roll(x, low_rank - 8 * b, 1)
        return jnp.where(l < rank + 8, pltpu.roll(x, low_rank - 8 * b, 1), pltpu.roll(x, low_rank + 8, 1))

    def stack(a, b):
        pad = jnp.zeros((ext - rank, 128), f32)
        return jnp.concatenate([a, pad, b, pad], axis=0)

    def finish(t, _):
        for g in range(half // 2):
            p0, p1 = accv[t, :, 256 * g:256 * g + 128], accv[t, :, 256 * g + 128:256 * g + 256]
            turning[g] = stack(*halves(p0, p1))
        for g in range(half // 2):
            turned = jnp.transpose(turning[g])
            for h in range(2):
                cols = slice((2 * g + h) * 128, (2 * g + h + 1) * 128)
                accv[t, :, cols] += turned[h * ext:h * ext + rank]
        for g in range(half):
            s = accv[t, :, g * 128:(g + 1) * 128]
            l = lax.rem(lax.broadcasted_iota(jnp.int32, (8, 128), 1), ext)
            for b in range(3):
                piece = jnp.where(l < rank, s[8 * b:8 * b + 8], spread(s[low_rank + 8 * b:low_rank + 8 * b + 8], b))
                sv[pl.ds(8 * b * pitch + g, 8, stride=pitch), :] = piece
        wpitch = low_rank + 1
        for c in range(low_rank):
            sw[pl.ds(c, rank, stride=wpitch), :] = accw[t, :, c * 128:(c + 1) * 128]
        for c in range(low_rank):
            e0, e1 = halves(sw[pl.ds(2 * c * wpitch, low_rank), :], sw[pl.ds((2 * c + 1) * wpitch, low_rank), :])
            pk[pl.ds(c * ext, low_rank, stride=2), :] = e0
            pk[pl.ds(c * ext + 1, low_rank, stride=2), :] = e1
        for c in range(low_rank):
            accw[t, :, c * 128:(c + 1) * 128] += pk[c * ext:c * ext + rank, :]
        for m in range(rank // 4):
            first = 2 * m
            turning[m] = jnp.transpose(stack(accw[t, :, first * 128:(first + 1) * 128], accw[t, :, (first + 1) * 128:(first + 2) * 128]))
        for m in range(rank // 8):
            lo, hi = turning[m], turning[m + rank // 8]
            l = lax.rem(lax.broadcasted_iota(jnp.int32, (ext, 128), 1), ext)
            for h in range(2):
                r = 4 * m + h
                x = jnp.where(l < rank, lo[h * ext:(h + 1) * ext], spread(hi[h * ext:(h + 1) * ext], m // 2))
                e0, e1 = halves(sv[pl.ds(r * pitch, half), :], sv[pl.ds((r + 2) * pitch, half), :])
                at = (2 * m + h) * ext
                pk[pl.ds(at, half, stride=2), :] = e0
                pk[pl.ds(at + 1, half, stride=2), :] = e1
                tile = slice((2 * m + h) * 128, (2 * m + h + 1) * 128)
                out[pl.ds(pl.multiple_of(t * ext, ext), ext), tile] = pk[at:at + ext, :] + x
        return 0

    lax.fori_loop(0, nb, finish, 0)


def contract(blocks, ownership, basis):
    slots, ext, area = blocks.shape
    size, rank = basis.shape
    nb = size // ext
    half = ext // 2
    u = basis.reshape(nb, ext, rank)
    ut = jnp.swapaxes(u, 1, 2)
    utp = u.reshape(nb, half, 2, rank).transpose(0, 3, 2, 1).reshape(nb, rank, ext)
    ub = jnp.pad(u, ((0, 0), (0, 0), (0, ext - rank)))
    count = jnp.sum((ownership[:, 0] >= 0).astype(jnp.int32)).reshape(1)
    sm = pl.BlockSpec(memory_space=pltpu.SMEM)
    vm = pl.BlockSpec(memory_space=pltpu.VMEM)
    return pl.pallas_call(
        functools.partial(contract_kernel, nb, ext, rank),
        out_shape=jax.ShapeDtypeStruct((size, rank // 2 * ext), f32),
        in_specs=[sm, sm, pl.BlockSpec(memory_space=pl.ANY), vm, vm, vm],
        out_specs=vm,
        scratch_shapes=[
            pltpu.VMEM((nb, rank, area), f32),
            pltpu.VMEM((nb, rank, rank * ext), f32),
            pltpu.VMEM((DEPTH, ext, area), bf16),
            pltpu.SemaphoreType.DMA((DEPTH,)),
            pltpu.VMEM((nb, 4 * ext, 4 * ext), bf16),
            pltpu.VMEM((3, ext, area), bf16),
            pltpu.VMEM((ext * (half + 1), 128), f32),
            pltpu.VMEM((rank * (half + 1), 128), f32),
            pltpu.VMEM((ext, area), bf16),
            pltpu.VMEM((rank // 2 * ext, 128), f32),
            pltpu.VMEM((half // 2, 128, 128), f32),
        ],
        compiler_params=pltpu.CompilerParams(vmem_limit_bytes=60 << 20),
    )(ownership.reshape(-1), count, blocks, ut, utp, ub)


def exchange_kernel(sizes, ext, part, y, out, near, ours, far, line, total, every, s_near, r_near, s_far, r_far, s_line, r_line, s_pair, r_pair, s_side, r_side, s_row, r_row):
    nx, nz, ng, rows, cols = sizes
    gx, gy, gz = lax.axis_index("gx"), lax.axis_index("gy"), lax.axis_index("gz")
    gh, core = gz // 2, lax.rem(gz, 2)
    side = [(a, b) for a in range(nx) for b in range(ng)]
    steps = side[1:] + side[:1]
    mate = (gx, gy, 2 * gh + 1 - core)

    def across(a, b):
        return lax.rem(gx + a, nx), lax.rem(gh + b, ng)

    def back(a, b):
        return lax.rem(gx + nx - a, nx), lax.rem(gh + ng - b, ng)

    def ahead(c):
        return lax.rem(gy + c, nz)

    def behind(c):
        return lax.rem(gy + nz - c, nz)

    def copy(src, dst, send, recv, device):
        return pltpu.make_async_remote_copy(
            src_ref=src, dst_ref=dst, send_sem=send, recv_sem=recv, device_id=device, device_id_type=MESH
        )

    def at_side(a, b):
        x, g = across(a, b)
        return (x, gy, 2 * g + core)

    def at_line(c):
        return (gx, ahead(c), gz)

    barrier = pltpu.get_barrier_semaphore()
    peers = [mate] + [at_side(a, b) for a, b in side[1:]] + [at_line(c) for c in range(1, nz)]
    for peer in peers:
        pl.semaphore_signal(barrier, inc=1, device_id=peer, device_id_type=MESH)
    pl.semaphore_wait(barrier, len(peers))

    pair = []
    for a, b in steps:
        x, g = across(a, b)
        m = a * ng + b
        c = copy(y.at[x, :, g, 1 - core], near.at[m], s_near.at[m], r_near.at[m], mate)
        c.start()
        pair.append(c)
    sent = []
    for (a, b), c in zip(steps, pair):
        x, g = across(a, b)
        m = a * ng + b
        c.wait_recv()
        for z in range(nz):
            ours[m, z] = (y[x, z, g, core] + near[m, z]).astype(bf16)
        if m:
            c = copy(ours.at[m], far.at[m], s_far.at[m], r_far.at[m], at_side(a, b))
            c.start()
            sent.append(c)
    for c in sent:
        c.wait_recv()
    hops = []
    for c in list(range(1, nz)) + [0]:
        z = ahead(c)
        t = ours[0, z].astype(f32)
        for m in range(1, len(side)):
            t = t + far[m, z].astype(f32)
        if c:
            line[c] = t.astype(bf16)
            d = copy(line.at[c], total.at[c], s_line.at[c], r_line.at[c], at_line(c))
            d.start()
            hops.append(d)
    for d in hops:
        d.wait_recv()
    for c in range(1, nz):
        t = t + total[c].astype(f32)
    mine = t.astype(bf16)

    def place(x, z, g, k):
        return ((x * nz + z) * ng + g) * 2 + k

    me = place(gx, gy, gh, core)
    every[me] = mine
    outgoing = []

    def send(where, sems, index, device):
        c = copy(every.at[where], every.at[where], sems[0].at[index], sems[1].at[index], device)
        c.start()
        outgoing.append(c)

    def landed(where, sems, index, device):
        copy(every.at[where], every.at[where], sems[0].at[index], sems[1].at[index], device).wait_recv()

    lines, sides, pairs = (s_row, r_row), (s_side, r_side), (s_pair, r_pair)
    for c in range(1, nz):
        send(me, lines, c, at_line(c))
    for m, (a, b) in enumerate(side[1:], 1):
        send(me, sides, m, at_side(a, b))
    send(me, pairs, 0, mate)
    for c in range(1, nz):
        where = place(gx, behind(c), gh, core)
        landed(where, lines, c, at_line(c))
        for m, (a, b) in enumerate(side[1:], 1):
            send(where, sides, c * len(side) + m, at_side(a, b))
        send(where, pairs, c * len(side), mate)
    for c in range(nz):
        for m, (a, b) in enumerate(side[1:], 1):
            x, g = back(a, b)
            where = place(x, behind(c), g, core)
            landed(where, sides, c * len(side) + m, at_side(a, b))
            send(where, pairs, c * len(side) + m, mate)
    for c in range(nz):
        for m, (a, b) in enumerate(side):
            x, g = back(a, b)
            landed(place(x, behind(c), g, 1 - core), pairs, c * len(side) + m, mate)
    for c in pair + sent + hops + outgoing:
        c.wait_send()

    l = lax.rem(lax.broadcasted_iota(jnp.int32, (rows, cols), 1), ext)
    once = (l < part) | ((l >= 2 * part) & (l < 2 * part + 8))
    weighted = (mine.astype(f32) * jnp.where(once, 1.0, 2.0)).astype(bf16)
    group = min(every.shape[0], 256 // rows)
    for first in range(0, every.shape[0], group):
        right = every[first:first + group].reshape(group * rows, cols)
        out[:, first * rows:(first + group) * rows] = lax.dot_general(
            weighted, right, (((1,), (1,)), ((), ())), preferred_element_type=f32
        )


def exchange(y, mesh_sizes, ext, part):
    x, z, g2 = mesh_sizes
    g = g2 // 2
    size, cols = y.shape
    devices = x * z * g2
    rows = size // devices
    m = x * g
    vm = pl.BlockSpec(memory_space=pltpu.VMEM)
    dma = lambda n: pltpu.SemaphoreType.DMA((n,))
    return pl.pallas_call(
        functools.partial(exchange_kernel, (x, z, g, rows, cols), ext, part),
        out_shape=jax.ShapeDtypeStruct((rows, size), f32),
        in_specs=[vm],
        out_specs=vm,
        scratch_shapes=[
            pltpu.VMEM((m, z, rows, cols), f32),
            pltpu.VMEM((m, z, rows, cols), bf16),
            pltpu.VMEM((m, z, rows, cols), bf16),
            pltpu.VMEM((z, rows, cols), bf16),
            pltpu.VMEM((z, rows, cols), bf16),
            pltpu.VMEM((devices, rows, cols), bf16),
            dma(m), dma(m), dma(m), dma(m), dma(z), dma(z),
            dma(z * m), dma(z * m), dma(z * m), dma(z * m), dma(z), dma(z),
        ],
        compiler_params=pltpu.CompilerParams(collective_id=0, has_side_effects=True, vmem_limit_bytes=48 << 20),
    )(y.reshape(x, z, g, 2, rows, cols))


def solution(mesh):
    sizes = tuple(mesh.shape[a] for a in AXES)

    def local(blocks, ownership, basis_rows):
        rank = basis_rows.shape[1]
        packed = contract(blocks, ownership, basis_rows)
        ext = blocks.shape[1]
        return exchange(packed, sizes, ext, rank // 2) / rank

    in_specs = (P(AXES, None, None), P(AXES, None), P())
    return jax.shard_map(local, mesh=mesh, in_specs=in_specs, out_specs=P(AXES, None), check_vma=False)
```

time: 819 us -> 150 us (0.18)
  matrix products: 359 us -> 0 us
  local copies, waits for them, and re-layouts: 250 us -> 4.97 us
  Pallas kernels: 0 us -> 141 us
  blocking collectives: 90.6 us -> 0 us
  waiting for transfers between devices: 58.2 us -> 0 us
  other arithmetic: 43.4 us -> 2 us
  between operations: 13.4 us -> 0.03 us
    dot_general x21 -> x0, matrix products: 359 us -> none  [the longest x15 211 us: reduce(): jnp.einsum(form, tensor * weights, factor, preferred_element_type=jnp.flo...]
    pallas_call x0 -> x2, Pallas kernels: none -> 141 us  [the longest x1 80.9 us: contract(): pl.pallas_call(functools.partial(contract_kernel, nb, ext, rank), out_sha...]
    dot_general x15 -> x0, local copies, waits for them, and re-layouts: 109 us -> none  [reduce(): jnp.einsum(form, tensor * weights, factor, preferred_element_type=jnp.flo...]
    all_to_all x1 -> x0, blocking collectives: 90.6 us -> none  [local(): lax.all_to_all(packed.reshape(devices, size // devices, -1), AXES, split_...]
    reshape x7 -> x2, local copies, waits for them, and re-layouts: 88.3 us -> 1.5 us  [the longest x1 0.82 us: contract(): u.reshape(nb, half, 2, rank).transpose(0, 3, 2, 1).reshape(nb, rank, ext)]
    all_gather x1 -> x0, waiting for transfers between devices: 58.2 us -> none  [local(): lax.all_gather(rounded, AXES, axis=0, tiled=True)]
    dynamic_slice x5 -> x0, local copies, waits for them, and re-layouts: 27.1 us -> none  [add_group(): stored = lax.dynamic_slice_in_dim(blocks, first_slot, group, 0)]
    another operation x1 -> x0, other arithmetic: 15.7 us -> none
  transfers between devices with their start and end apart: 1 -> 0, of which waited for: 1 -> 0; matrix products, arithmetic and copies ran while one was open for 0% -> 0% of each run, Pallas kernels for 0% -> 0%
where the time goes in v1:
time: 150 us; the launch traced here: 148 us
  Pallas kernels  141 us (94%)
  local copies, waits for them, and re-layouts  4.97 us (3%)
  other arithmetic  2 us (1%)
    pallas_call x1, Pallas kernels, contract(): pl.pallas_call(functools.partial(contract_kernel, nb, ext, rank), out_sha...  80.9 us
    pallas_call x1, Pallas kernels, exchange(): pl.pallas_call(functools.partial(exchange_kernel, (x, z, g, rows, cols),...  59.9 us

profile of v1, /device:TPU:0, one launch (start us, length us, event | category | flops | bytes accessed | tf_op | source)
XLA Modules:
  0.0 147.9 jit_solution(3626335378930294449)
XLA Ops:
  0.0 1.3 fusion
  1.3 0.8 copy.7
  2.1 0.7 reshape.18.own
  2.8 1.1 copy.8
  3.9 0.8 copy.11.ut
  4.7 0.8 pad.4.ub
  5.5 0.8 copy.12.utp
  6.3 80.9 %shard_map.37 = f32[1024,1536]{1,0:T(8,128)} custom-call(s32[150]{0:T(256)} %reshape.18.own, s32[1]{0:T(128)} %bitcast.count, bf16[50,64,4096]{2,1,0:T(8,128)(2,1)} %blocks.1, bf16[16,48,64]{2,1,0:T(8,128)(2,1)} %copy.11.ut, bf16[16,48,64]{2,1,0:T(8,128)(2,1)} %copy.12.utp, bf16[16,64,64]{2,1,0:T(8,128)(2,1)} %pad.4.ub), custom_call_target="tpu_custom_call" | custom-call | tf_op jit(solution)/shard_map/pallas_call | solution.py:176
  87.3 59.9 %shard_map.38 = f32[32,1024]{1,0:T(8,128)S(1)} custom-call(f32[2,4,2,2,32,1536]{5,4,3,2,1,0:T(8,128)} %bitcast.9), custom_call_target="tpu_custom_call" | custom-call | tf_op jit(solution)/shard_map/pallas_call | solution.py:333
  147.2 0.7 broadcast_multiply_fusion
  (1 shorter events, 0.0 us)

commit v2 on v1

--- a/solution.py
+++ b/solution.py
@@ -13,7 +13,7 @@
 MESH = pl.DeviceIdType.MESH
 
 
-def contract_kernel(nb, ext, rank, own, count, blocks, ut, utp, ub, out, accv, accw, buf, sems, bd, mask, sv, sw, vb, pk, turning):
+def contract_kernel(nb, ext, rank, own, count, blocks, ut, utp, ub, out, accv, accw, buf, sems, bd, mask, sv, sw, vb, pk, turning, ready, gone):
     half = ext // 2
     pitch = half + 1
     width = 4 * ext
@@ -117,7 +117,16 @@
         pad = jnp.zeros((ext - rank, 128), f32)
         return jnp.concatenate([a, pad, b, pad], axis=0)
 
+    def leave(t):
+        slot = lax.rem(t, 2)
+        return pltpu.make_async_copy(ready.at[slot], out.at[pl.ds(pl.multiple_of(t * ext, ext), ext), :], gone.at[slot])
+
     def finish(t, _):
+        @pl.when(t >= 2)
+        def _():
+            leave(t - 2).wait()
+
+        slot = lax.rem(t, 2)
         for g in range(half // 2):
             p0, p1 = accv[t, :, 256 * g:256 * g + 128], accv[t, :, 256 * g + 128:256 * g + 256]
             turning[g] = stack(*halves(p0, p1))
@@ -155,10 +164,13 @@
                 pk[pl.ds(at, half, stride=2), :] = e0
                 pk[pl.ds(at + 1, half, stride=2), :] = e1
                 tile = slice((2 * m + h) * 128, (2 * m + h + 1) * 128)
-                out[pl.ds(pl.multiple_of(t * ext, ext), ext), tile] = pk[at:at + ext, :] + x
+                ready[slot, :, tile] = pk[at:at + ext, :] + x
+        leave(t).start()
         return 0
 
     lax.fori_loop(0, nb, finish, 0)
+    for t in range(max(nb - 2, 0), nb):
+        leave(t).wait()
 
 
 def contract(blocks, ownership, basis):
@@ -177,7 +189,7 @@
         functools.partial(contract_kernel, nb, ext, rank),
         out_shape=jax.ShapeDtypeStruct((size, rank // 2 * ext), f32),
         in_specs=[sm, sm, pl.BlockSpec(memory_space=pl.ANY), vm, vm, vm],
-        out_specs=vm,
+        out_specs=pl.BlockSpec(memory_space=pl.ANY),
         scratch_shapes=[
             pltpu.VMEM((nb, rank, area), f32),
             pltpu.VMEM((nb, rank, rank * ext), f32),
@@ -190,12 +202,14 @@
             pltpu.VMEM((ext, area), bf16),
             pltpu.VMEM((rank // 2 * ext, 128), f32),
             pltpu.VMEM((half // 2, 128, 128), f32),
+            pltpu.VMEM((2, ext, rank // 2 * ext), f32),
+            pltpu.SemaphoreType.DMA((2,)),
         ],
         compiler_params=pltpu.CompilerParams(vmem_limit_bytes=60 << 20),
     )(ownership.reshape(-1), count, blocks, ut, utp, ub)
 
 
-def exchange_kernel(sizes, ext, part, y, out, near, ours, far, line, total, every, s_near, r_near, s_far, r_far, s_line, r_line, s_pair, r_pair, s_side, r_side, s_row, r_row):
+def exchange_kernel(sizes, ext, part, y, out, kept, near, ours, far, line, total, every, s_kept, s_near, r_near, s_far, r_far, s_line, r_line, s_pair, r_pair, s_side, r_side, s_row, r_row):
     nx, nz, ng, rows, cols = sizes
     gx, gy, gz = lax.axis_index("gx"), lax.axis_index("gy"), lax.axis_index("gz")
     gh, core = gz // 2, lax.rem(gz, 2)
@@ -233,40 +247,37 @@
         pl.semaphore_signal(barrier, inc=1, device_id=peer, device_id_type=MESH)
     pl.semaphore_wait(barrier, len(peers))
 
-    pair = []
-    for a, b in steps:
-        x, g = across(a, b)
-        m = a * ng + b
-        c = copy(y.at[x, :, g, 1 - core], near.at[m], s_near.at[m], r_near.at[m], mate)
-        c.start()
-        pair.append(c)
-    sent = []
-    for (a, b), c in zip(steps, pair):
-        x, g = across(a, b)
-        m = a * ng + b
-        c.wait_recv()
-        for z in range(nz):
-            ours[m, z] = (y[x, z, g, core] + near[m, z]).astype(bf16)
-        if m:
-            c = copy(ours.at[m], far.at[m], s_far.at[m], r_far.at[m], at_side(a, b))
-            c.start()
-            sent.append(c)
-    for c in sent:
-        c.wait_recv()
-    hops = []
-    for c in list(range(1, nz)) + [0]:
-        z = ahead(c)
-        t = ours[0, z].astype(f32)
-        for m in range(1, len(side)):
-            t = t + far[m, z].astype(f32)
+    order = list(range(1, nz)) + [0]
+    wide = len(side)
+    own, pair = {}, {}
+    for c in order:
+        pair[c] = copy(y.at[:, ahead(c), :, 1 - core], near.at[c], s_near.at[c], r_near.at[c], mate)
+        pair[c].start()
+        own[c] = pltpu.make_async_copy(y.at[:, ahead(c), :, core], kept.at[c], s_kept.at[c])
+        own[c].start()
+    sent = {}
+    for c in order:
+        own[c].wait()
+        pair[c].wait_recv()
+        for m, (a, b) in enumerate(steps, 1):
+            m = m % wide
+            x, g = across(a, b)
+            ours[m, c] = (kept[c, x, g] + near[c, x, g]).astype(bf16)
+            if m:
+                sent[m, c] = copy(ours.at[m, c], far.at[m, c], s_far.at[m * nz + c], r_far.at[m * nz + c], at_side(a, b))
+                sent[m, c].start()
+    hops = {}
+    for c in order:
+        t = ours[0, c].astype(f32)
+        for m in range(1, wide):
+            sent[m, c].wait_recv()
+            t = t + far[m, c].astype(f32)
         if c:
             line[c] = t.astype(bf16)
-            d = copy(line.at[c], total.at[c], s_line.at[c], r_line.at[c], at_line(c))
-            d.start()
-            hops.append(d)
-    for d in hops:
-        d.wait_recv()
+            hops[c] = copy(line.at[c], total.at[c], s_line.at[c], r_line.at[c], at_line(c))
+            hops[c].start()
     for c in range(1, nz):
+        hops[c].wait_recv()
         t = t + total[c].astype(f32)
     mine = t.astype(bf16)
 
@@ -282,32 +293,54 @@
         c.start()
         outgoing.append(c)
 
-    def landed(where, sems, index, device):
-        copy(every.at[where], every.at[where], sems[0].at[index], sems[1].at[index], device).wait_recv()
+    def landed(where, sems, index):
+        copy(every.at[where], every.at[where], sems[0].at[index], sems[1].at[index], mate).wait_recv()
 
     lines, sides, pairs = (s_row, r_row), (s_side, r_side), (s_pair, r_pair)
+    straight = [(m, a, b) for m, (a, b) in enumerate(side) if (a == 0) != (b == 0)]
+    corner = [(m, a, b) for m, (a, b) in enumerate(side) if a and b]
+
+    def origin(c, a, b, k):
+        x, g = back(a, b)
+        return place(x, behind(c), g, k)
+
+    def hand_out(c):
+        where = origin(c, 0, 0, core)
+        for m, a, b in straight:
+            send(where, sides, c * wide + m, at_side(a, b))
+        send(where, pairs, c * wide, mate)
+
+    def relay(c):
+        for m, a, b in straight:
+            where = origin(c, a, b, core)
+            landed(where, sides, c * wide + m)
+            if a and c % 2 == 0:
+                for o, (p, q) in enumerate(side):
+                    if p == a and q:
+                        send(where, sides, c * wide + o, at_side(0, q))
+            if b and c % 2 == 1:
+                for o, (p, q) in enumerate(side):
+                    if q == b and p:
+                        send(where, sides, c * wide + o, at_side(p, 0))
+            send(where, pairs, c * wide + m, mate)
+
     for c in range(1, nz):
         send(me, lines, c, at_line(c))
-    for m, (a, b) in enumerate(side[1:], 1):
-        send(me, sides, m, at_side(a, b))
-    send(me, pairs, 0, mate)
-    for c in range(1, nz):
-        where = place(gx, behind(c), gh, core)
-        landed(where, lines, c, at_line(c))
-        for m, (a, b) in enumerate(side[1:], 1):
-            send(where, sides, c * len(side) + m, at_side(a, b))
-        send(where, pairs, c * len(side), mate)
+    hand_out(0)
+    for c in range(1, nz + 1):
+        if c < nz:
+            landed(origin(c, 0, 0, core), lines, c)
+            hand_out(c)
+        relay(c - 1)
     for c in range(nz):
-        for m, (a, b) in enumerate(side[1:], 1):
-            x, g = back(a, b)
-            where = place(x, behind(c), g, core)
-            landed(where, sides, c * len(side) + m, at_side(a, b))
-            send(where, pairs, c * len(side) + m, mate)
+        for m, a, b in corner:
+            where = origin(c, a, b, core)
+            landed(where, sides, c * wide + m)
+            send(where, pairs, c * wide + m, mate)
     for c in range(nz):
         for m, (a, b) in enumerate(side):
-            x, g = back(a, b)
-            landed(place(x, behind(c), g, 1 - core), pairs, c * len(side) + m, mate)
-    for c in pair + sent + hops + outgoing:
+            landed(origin(c, a, b, 1 - core), pairs, c * wide + m)
+    for c in [*pair.values(), *sent.values(), *hops.values(), *outgoing]:
         c.wait_send()
 
     l = lax.rem(lax.broadcasted_iota(jnp.int32, (rows, cols), 1), ext)
@@ -333,16 +366,17 @@
     return pl.pallas_call(
         functools.partial(exchange_kernel, (x, z, g, rows, cols), ext, part),
         out_shape=jax.ShapeDtypeStruct((rows, size), f32),
-        in_specs=[vm],
+        in_specs=[pl.BlockSpec(memory_space=pl.ANY)],
         out_specs=vm,
         scratch_shapes=[
-            pltpu.VMEM((m, z, rows, cols), f32),
+            pltpu.VMEM((z, x, g, rows, cols), f32),
+            pltpu.VMEM((z, x, g, rows, cols), f32),
             pltpu.VMEM((m, z, rows, cols), bf16),
             pltpu.VMEM((m, z, rows, cols), bf16),
             pltpu.VMEM((z, rows, cols), bf16),
             pltpu.VMEM((z, rows, cols), bf16),
             pltpu.VMEM((devices, rows, cols), bf16),
-            dma(m), dma(m), dma(m), dma(m), dma(z), dma(z),
+            dma(z), dma(z), dma(z), dma(m * z), dma(m * z), dma(z), dma(z),
             dma(z * m), dma(z * m), dma(z * m), dma(z * m), dma(z), dma(z),
         ],
         compiler_params=pltpu.CompilerParams(collective_id=0, has_side_effects=True, vmem_limit_bytes=48 << 20),

time: 150 us -> 136 us (0.907)
  Pallas kernels: 141 us -> 128 us
    pallas_call x1, Pallas kernels: 59.9 us -> 49.2 us  [exchange(): pl.pallas_call(functools.partial(exchange_kernel, (x, z, g, rows, cols),...]
    pallas_call x1, Pallas kernels: 80.9 us -> 78.8 us  [contract(): pl.pallas_call(functools.partial(contract_kernel, nb, ext, rank), out_sha...]
where the time goes in v2:
time: 136 us; the launch traced here: 135 us
  Pallas kernels  128 us (94%)
  local copies, waits for them, and re-layouts  4.97 us (4%)
  other arithmetic  2 us (1%)
    pallas_call x1, Pallas kernels, contract(): pl.pallas_call(functools.partial(contract_kernel, nb, ext, rank), out_sha...  78.8 us
    pallas_call x1, Pallas kernels, exchange(): pl.pallas_call(functools.partial(exchange_kernel, (x, z, g, rows, cols),...  49.2 us

profile of v2, /device:TPU:0, one launch (start us, length us, event | category | flops | bytes accessed | tf_op | source)
XLA Modules:
  0.0 135.0 jit_solution(17740440217482607581)
XLA Ops:
  0.0 1.3 fusion
  1.3 0.8 copy.7
  2.1 0.7 reshape.18.own
  2.8 1.1 copy.8
  3.9 0.8 copy.11.ut
  4.7 0.8 pad.4.ub
  5.5 0.8 copy.12.utp
  6.3 78.8 %shard_map.37 = f32[1024,1536]{1,0:T(8,128)} custom-call(s32[150]{0:T(256)} %reshape.18.own, s32[1]{0:T(128)} %bitcast.count, bf16[50,64,4096]{2,1,0:T(8,128)(2,1)} %blocks.1, bf16[16,48,64]{2,1,0:T(8,128)(2,1)} %copy.11.ut, bf16[16,48,64]{2,1,0:T(8,128)(2,1)} %copy.12.utp, bf16[16,64,64]{2,1,0:T(8,128)(2,1)} %pad.4.ub), custom_call_target="tpu_custom_call" | custom-call | tf_op jit(solution)/shard_map/pallas_call | solution.py:188
  85.1 49.2 %shard_map.38 = f32[32,1024]{1,0:T(8,128)S(1)} custom-call(f32[2,4,2,2,32,1536]{5,4,3,2,1,0:T(8,128)} %bitcast.9), custom_call_target="tpu_custom_call" | custom-call | tf_op jit(solution)/shard_map/pallas_call | solution.py:366
  134.3 0.7 broadcast_multiply_fusion
  (1 shorter events, 0.0 us)

commit v3 on v2

--- a/solution.py
+++ b/solution.py
@@ -13,13 +13,13 @@
 MESH = pl.DeviceIdType.MESH
 
 
-def contract_kernel(nb, ext, rank, own, count, blocks, ut, utp, ub, out, accv, accw, buf, sems, bd, mask, sv, sw, vb, pk, turning, ready, gone):
+def contract_kernel(nb, ext, rank, own, blocks, ut, utp, ub, out, accv, accw, buf, sems, bd, mask, sv, sw, vb, pk, turning, turned2, ready, gone):
     half = ext // 2
     pitch = half + 1
     width = 4 * ext
     chunks = ext * ext // width
     low_rank = rank // 2
-    n = count[0]
+    n = lax.fori_loop(0, own.shape[0], lambda s, found: found + jnp.where(own[s, 0] >= 0, 1, 0), 0)
 
     def fetch(s):
         return pltpu.make_async_copy(blocks.at[s], buf.at[lax.rem(s, DEPTH)], sems.at[lax.rem(s, DEPTH)])
@@ -70,7 +70,7 @@
         def _():
             fetch(s + DEPTH - 1).start()
 
-        i, j, k = own[3 * s], own[3 * s + 1], own[3 * s + 2]
+        i, j, k = own[s, 0], own[s, 1], own[s, 2]
         kind = jnp.where(j == k, jnp.where(i == j, 2, 1), 0)
 
         @pl.when((i == j) | (j == k))
@@ -82,16 +82,19 @@
         ui = ut[i]
         uj = utp[j]
         bdk = bd[k]
-        for c in range(chunks):
-            cols = slice(c * width, (c + 1) * width)
-            t = buf[cur, :, cols]
-            v = jnp.dot(t, bdk, preferred_element_type=f32)
-            sv[pl.ds(2 * c, ext, stride=pitch), :] = v[:, :128]
-            sv[pl.ds(2 * c + 1, ext, stride=pitch), :] = v[:, 128:]
-            vb[:, cols] = v.astype(bf16)
-            w = jnp.dot(ui, t, preferred_element_type=f32)
-            sw[pl.ds(2 * c, rank, stride=pitch), :] = w[:, :128]
-            sw[pl.ds(2 * c + 1, rank, stride=pitch), :] = w[:, 128:]
+        for first in range(0, chunks, 4):
+            group = range(first, first + 4)
+            t = {c: buf[cur, :, c * width:(c + 1) * width] for c in group}
+            v4 = jnp.dot(jnp.concatenate([t[c] for c in group], axis=0), bdk, preferred_element_type=f32)
+            for c in group:
+                v = v4[(c - first) * ext:(c - first + 1) * ext]
+                sv[pl.ds(2 * c, ext, stride=pitch), :] = v[:, :128]
+                sv[pl.ds(2 * c + 1, ext, stride=pitch), :] = v[:, 128:]
+                vb[:, c * width:(c + 1) * width] = v.astype(bf16)
+            for c in group:
+                w = jnp.dot(ui, t[c], preferred_element_type=f32)
+                sw[pl.ds(2 * c, rank, stride=pitch), :] = w[:, :128]
+                sw[pl.ds(2 * c + 1, rank, stride=pitch), :] = w[:, 128:]
         for c in range(chunks):
             cols = slice(c * width, (c + 1) * width)
             accv[j, :, cols] += jnp.dot(ui, vb[:, cols], preferred_element_type=f32)
@@ -127,20 +130,6 @@
             leave(t - 2).wait()
 
         slot = lax.rem(t, 2)
-        for g in range(half // 2):
-            p0, p1 = accv[t, :, 256 * g:256 * g + 128], accv[t, :, 256 * g + 128:256 * g + 256]
-            turning[g] = stack(*halves(p0, p1))
-        for g in range(half // 2):
-            turned = jnp.transpose(turning[g])
-            for h in range(2):
-                cols = slice((2 * g + h) * 128, (2 * g + h + 1) * 128)
-                accv[t, :, cols] += turned[h * ext:h * ext + rank]
-        for g in range(half):
-            s = accv[t, :, g * 128:(g + 1) * 128]
-            l = lax.rem(lax.broadcasted_iota(jnp.int32, (8, 128), 1), ext)
-            for b in range(3):
-                piece = jnp.where(l < rank, s[8 * b:8 * b + 8], spread(s[low_rank + 8 * b:low_rank + 8 * b + 8], b))
-                sv[pl.ds(8 * b * pitch + g, 8, stride=pitch), :] = piece
         wpitch = low_rank + 1
         for c in range(low_rank):
             sw[pl.ds(c, rank, stride=wpitch), :] = accw[t, :, c * 128:(c + 1) * 128]
@@ -148,13 +137,27 @@
             e0, e1 = halves(sw[pl.ds(2 * c * wpitch, low_rank), :], sw[pl.ds((2 * c + 1) * wpitch, low_rank), :])
             pk[pl.ds(c * ext, low_rank, stride=2), :] = e0
             pk[pl.ds(c * ext + 1, low_rank, stride=2), :] = e1
+        for g in range(half // 2):
+            p0, p1 = accv[t, :, 256 * g:256 * g + 128], accv[t, :, 256 * g + 128:256 * g + 256]
+            turning[g] = stack(*halves(p0, p1))
         for c in range(low_rank):
             accw[t, :, c * 128:(c + 1) * 128] += pk[c * ext:c * ext + rank, :]
+        for g in range(half // 2):
+            turned = jnp.transpose(turning[g])
+            for h in range(2):
+                cols = slice((2 * g + h) * 128, (2 * g + h + 1) * 128)
+                accv[t, :, cols] += turned[h * ext:h * ext + rank]
         for m in range(rank // 4):
             first = 2 * m
-            turning[m] = jnp.transpose(stack(accw[t, :, first * 128:(first + 1) * 128], accw[t, :, (first + 1) * 128:(first + 2) * 128]))
+            turned2[m] = jnp.transpose(stack(accw[t, :, first * 128:(first + 1) * 128], accw[t, :, (first + 1) * 128:(first + 2) * 128]))
+        for g in range(half):
+            s = accv[t, :, g * 128:(g + 1) * 128]
+            l = lax.rem(lax.broadcasted_iota(jnp.int32, (8, 128), 1), ext)
+            for b in range(3):
+                piece = jnp.where(l < rank, s[8 * b:8 * b + 8], spread(s[low_rank + 8 * b:low_rank + 8 * b + 8], b))
+                sv[pl.ds(8 * b * pitch + g, 8, stride=pitch), :] = piece
         for m in range(rank // 8):
-            lo, hi = turning[m], turning[m + rank // 8]
+            lo, hi = turned2[m], turned2[m + rank // 8]
             l = lax.rem(lax.broadcasted_iota(jnp.int32, (ext, 128), 1), ext)
             for h in range(2):
                 r = 4 * m + h
@@ -182,13 +185,12 @@
     ut = jnp.swapaxes(u, 1, 2)
     utp = u.reshape(nb, half, 2, rank).transpose(0, 3, 2, 1).reshape(nb, rank, ext)
     ub = jnp.pad(u, ((0, 0), (0, 0), (0, ext - rank)))
-    count = jnp.sum((ownership[:, 0] >= 0).astype(jnp.int32)).reshape(1)
     sm = pl.BlockSpec(memory_space=pltpu.SMEM)
     vm = pl.BlockSpec(memory_space=pltpu.VMEM)
     return pl.pallas_call(
         functools.partial(contract_kernel, nb, ext, rank),
         out_shape=jax.ShapeDtypeStruct((size, rank // 2 * ext), f32),
-        in_specs=[sm, sm, pl.BlockSpec(memory_space=pl.ANY), vm, vm, vm],
+        in_specs=[sm, pl.BlockSpec(memory_space=pl.ANY), vm, vm, vm],
         out_specs=pl.BlockSpec(memory_space=pl.ANY),
         scratch_shapes=[
             pltpu.VMEM((nb, rank, area), f32),
@@ -202,11 +204,12 @@
             pltpu.VMEM((ext, area), bf16),
             pltpu.VMEM((rank // 2 * ext, 128), f32),
             pltpu.VMEM((half // 2, 128, 128), f32),
+            pltpu.VMEM((rank // 4, 128, 128), f32),
             pltpu.VMEM((2, ext, rank // 2 * ext), f32),
             pltpu.SemaphoreType.DMA((2,)),
         ],
         compiler_params=pltpu.CompilerParams(vmem_limit_bytes=60 << 20),
-    )(ownership.reshape(-1), count, blocks, ut, utp, ub)
+    )(ownership, blocks, ut, utp, ub)
 
 
 def exchange_kernel(sizes, ext, part, y, out, kept, near, ours, far, line, total, every, s_kept, s_near, r_near, s_far, r_far, s_line, r_line, s_pair, r_pair, s_side, r_side, s_row, r_row):

time: 136 us -> 125 us (0.919)
  Pallas kernels: 128 us -> 120 us
    pallas_call x1, Pallas kernels: 78.8 us -> 70 us  [contract(): pl.pallas_call(functools.partial(contract_kernel, nb, ext, rank), out_sha...]
where the time goes in v3:
time: 125 us
  Pallas kernels  120 us (96%)
  local copies, waits for them, and re-layouts  4.89 us (4%)
    pallas_call x1, Pallas kernels, contract(): pl.pallas_call(functools.partial(contract_kernel, nb, ext, rank), out_sha...  70 us
    pallas_call x1, Pallas kernels, exchange(): pl.pallas_call(functools.partial(exchange_kernel, (x, z, g, rows, cols),...  49.7 us

profile of v3, /device:TPU:0, one launch (start us, length us, event | category | flops | bytes accessed | tf_op | source)
XLA Modules:
  0.0 125.4 jit_solution(16113195300756571097)
XLA Ops:
  0.0 1.4 %copy.11.own = s32[50,3]{1,0:T(8,128)} copy(s32[50,3]{0,1:T(4,128)} %param.4) | data formatting | bytes 1200 | tf_op args[1]
  1.4 1.1 copy.8
  2.4 0.8 copy.12.ut
  3.3 0.8 pad.4.ub
  4.1 0.8 copy.13.utp
  4.9 70.0 %shard_map.37 = f32[1024,1536]{1,0:T(8,128)} custom-call(s32[50,3]{1,0:T(8,128)} %copy.11.own, bf16[50,64,4096]{2,1,0:T(8,128)(2,1)} %blocks.1, bf16[16,48,64]{2,1,0:T(8,128)(2,1)} %copy.12.ut, bf16[16,48,64]{2,1,0:T(8,128)(2,1)} %copy.13.utp, bf16[16,64,64]{2,1,0:T(8,128)(2,1)} %pad.4.ub), custom_call_target="tpu_custom_call" | custom-call | tf_op jit(solution)/shard_map/pallas_call | solution.py:190
  75.0 49.7 %shard_map.38 = f32[32,1024]{1,0:T(8,128)S(1)} custom-call(f32[2,4,2,2,32,1536]{5,4,3,2,1,0:T(8,128)} %bitcast.8), custom_call_target="tpu_custom_call" | custom-call | tf_op jit(solution)/shard_map/pallas_call | solution.py:369
  124.7 0.7 broadcast_multiply_fusion
  (1 shorter events, 0.0 us)
